TPU v7x, 32 devices: a whole 2x2x4 slice. The times are simulated.
32 devices in a mesh: row: 8 (over y, x, core), col: 4 (over z).
Axes of the slice: x: 2, y: 2, z: 4, core: 2. Of those that a mesh axis runs over, the one named last changes fastest.
Arguments:
- src_points: bfloat16 [8192, 256], P('row'), may hold values from -32 to 32, as said below
- tgt_points: bfloat16 [16384, 256], P(('col', 'row')), may hold values from -32 to 32, as said below
- log_src_mass: float32 [8192], P('row'), may hold values from -3 to 3
- log_tgt_mass: float32 [16384], P('col'), may hold values from -3 to 3
Outputs:
- src_potential: float32 [8192], P('row')
- tgt_potential: float32 [16384], P('col')
- mean_potentials: float32 [], replicated
Inputs may be any that keep to these rules, and one draw needn't show every extreme that they name: `src_points`: point coordinates. `tgt_points`: point coordinates.
All inputs are finite; a program needn't handle non-finite values.
Results may differ from a plain program's by a relative error of at most 0.0003.
Values may be sent and summed in bfloat16 or wider, within the bound.
A program may use at most 64 MiB of HBM per device.

v0:
```python
import jax
import jax.numpy as jnp
from jax import lax
from jax.sharding import PartitionSpec as P

ITERS = 3


entropy_weight = 0.1


def combined_all(value, axis, combine):
    everything = jax.tree.map(lambda part: lax.all_gather(part, axis), value)
    leading = jax.tree.map(lambda part: part[0], everything)

    def turn(k, so_far):
        return combine(so_far, jax.tree.map(lambda part: part[k], everything))

    return lax.fori_loop(1, lax.axis_size(axis), turn, leading)


def cost_block(points_a, squares_a, points_b, squares_b):
    product = lax.dot_general(
        points_a, points_b, (((1,), (1,)), ((), ())), preferred_element_type=jnp.float32
    )
    return (squares_a[:, None] + squares_b[None, :] - 2.0 * product) / points_a.shape[1]


def combine(early, later):
    top = jnp.maximum(early[0], later[0])
    return (top, early[1] * jnp.exp(early[0] - top) + later[1] * jnp.exp(later[0] - top))


def body(src_points, tgt_points, log_src_mass, log_tgt_mass):
    targets = lax.all_gather(tgt_points, "row", axis=0, tiled=True)
    sqy = jnp.sum(targets.astype(jnp.float32) ** 2, axis=1)
    count = src_points.shape[0]
    block = min(256, count)
    blocks = count // block
    src_blocks = src_points.reshape(blocks, block, -1)
    sq_blocks = jnp.sum(src_points.astype(jnp.float32) ** 2, axis=1).reshape(blocks, block)
    mass_blocks = log_src_mass.reshape(blocks, block)
    width_tgt = targets.shape[0]
    tgt_potential = jnp.zeros((width_tgt,), jnp.float32)
    src_potential = jnp.zeros((count,), jnp.float32)
    for step in range(ITERS):

        def row_terms(points, squares):
            cost = cost_block(points, squares, targets, sqy)
            return log_tgt_mass[None, :] + (tgt_potential[None, :] - cost) / entropy_weight

        def row_pair(item):
            terms = row_terms(item[0], item[1])
            top = jnp.max(terms, axis=1)
            return (top, jnp.sum(jnp.exp(terms - top[:, None]), axis=1))

        top, total = lax.map(row_pair, (src_blocks, sq_blocks))
        top, total = combined_all((top.reshape(-1), total.reshape(-1)), "col", combine)
        src_potential = -entropy_weight * (top + jnp.log(total))
        pot_blocks = src_potential.reshape(blocks, block)

        def col_terms(points, squares, mass, pot):
            cost = cost_block(points, squares, targets, sqy)
            return mass[:, None] + (pot[:, None] - cost) / entropy_weight

        def pair_step(carry, item):
            terms = col_terms(item[0], item[1], item[2], item[3])
            block_top = jnp.max(terms, axis=0)
            block_sum = jnp.sum(jnp.exp(terms - block_top[None, :]), axis=0)
            return (combine(carry, (block_top, block_sum)), None)

        start = (
            jnp.full((width_tgt,), -jnp.inf, jnp.float32),
            jnp.zeros((width_tgt,), jnp.float32),
        )
        inputs = (src_blocks, sq_blocks, mass_blocks, pot_blocks)
        (top, total), unused = lax.scan(pair_step, start, inputs)
        top, total = combined_all((top, total), "row", combine)
        tgt_potential = -entropy_weight * (top + jnp.log(total))
    sources_all = count * lax.axis_size("row")
    targets_all = width_tgt * lax.axis_size("col")
    local = jnp.sum(src_potential) / (sources_all * lax.axis_size("col")) + jnp.sum(
        tgt_potential
    ) / (targets_all * lax.axis_size("row"))
    mean_potentials = lax.psum(local, ("row", "col"))
    return (src_potential, tgt_potential, mean_potentials)


def solution(mesh):
    return jax.shard_map(
        body,
        mesh=mesh,
        in_specs=(P("row", None), P(("col", "row"), None), P("row"), P("col")),
        out_specs=(P("row"), P("col"), P()),
        check_vma=False,
    )
```

profile of v0, /device:TPU:0, one launch (start us, length us, event | category | flops | bytes accessed | tf_op | source)
XLA Modules:
  0.0 320.3 jit_solution(3803695196308315043)
XLA Ops:
  7.2 0.7 all-gather.14.cloned.1.call-update
  8.0 1.3 multiply_reduce_fusion.1
  9.2 0.7 reshape.65
  9.9 30.5 %all-gather.14.cloned.1.call-done = bf16[4096,256]{1,0:T(8,128)(2,1)} async-done(((bf16[512,256]{1,0:T(8,128)(2,1)}), bf16[4096,256]{1,0:T(8,128)(2,1)}) %all-gather.14.cloned.1.call-update) | async-done | bytes 2097168 | tf_op jit(solution)/shard_map/all_gather | solution.py:35
  40.4 2.2 multiply_reduce_fusion
  42.6 15.6 %while.177 = (s32[]{:T(128)}, f32[4,256]{1,0:T(4,128)S(1)}, f32[4,256]{1,0:T(4,128)S(1)}, f32[4096]{0:T(1024)}, f32[4,256]{1,0:T(4,128)S(1)}, /*index=5*/f32[409...) while((s32[]{:T(128)}, f32[4,256]{1,0:T(4,128)S(1)}, ...), condition=%wide.region_5.6_spmd, body=%wide.region_2.5_spmd.sunk | while | flops 547356160 | bytes 10660465 | solution.py:57
  42.7 3.1 fusion.81
  45.7 0.7 exponential_reduce_fusion.12
  46.6 3.1 fusion.81
  49.6 0.7 exponential_reduce_fusion.12
  50.5 3.1 fusion.81
  53.5 0.7 exponential_reduce_fusion.12
  54.4 3.1 fusion.81
  57.4 0.7 exponential_reduce_fusion.12
  58.3 13.3 %all-gather.6 = f32[4,1,1024]{2,1,0:T(1,128)S(1)} all-gather(f32[1,1,1024]{2,1,0:T(1,128)S(1)} %reshape.89), channel_id=1, replica_groups=mesh['row'=8,'col'=4] {'col'}, dimensions={0}, use_global_device_ids=true | all-gather | bytes 20480 | tf_op jit(solution)/shard_map/all_gather | solution.py:13
  71.5 13.2 %all-gather.7 = f32[4,1,1024]{2,1,0:T(1,128)S(1)} all-gather(f32[1,1,1024]{2,1,0:T(1,128)S(1)} %reshape.91), channel_id=1, replica_groups=mesh['row'=8,'col'=4] {'col'}, dimensions={0}, use_global_device_ids=true | all-gather | bytes 20480 | tf_op jit(solution)/shard_map/all_gather | solution.py:13
  85.0 15.2 %while.186 = (s32[]{:T(128)}, f32[4096]{0:T(1024)S(1)}, f32[4096]{0:T(1024)S(1)}, f32[4,256]{1,0:T(4,128)S(1)}, f32[4,256]{1,0:T(4,128)S(1)}, /*index=5*/f32[4,2...) while((s32[]{:T(128)}, f32[4096]{0:T(1024)S(1)}, ...), condition=%wide.region_11.12_spmd.clone, body=%wide.region_8.11_spmd.clone.sunk | while | flops 547381248 | bytes 10790527 | solution.py:77
  85.0 3.1 fusion.87
  88.2 0.6 exponential_reduce_fusion.15
  88.8 3.1 fusion.87
  92.6 3.1 fusion.87
  96.4 3.1 fusion.87
  99.6 0.6 exponential_reduce_fusion.15
  100.2 9.2 %all-gather = f32[32768]{0:T(1024)S(1)} all-gather(f32[4096]{0:T(1024)S(1)} %get-tuple-element.1088), channel_id=2, replica_groups=mesh['row'=8,'col'=4] {'row'}, dimensions={0}, use_global_device_ids=true | all-gather | bytes 147456 | tf_op jit(solution)/shard_map/all_gather | solution.py:13
  109.4 8.3 %all-gather.1 = f32[32768]{0:T(1024)S(1)} all-gather(f32[4096]{0:T(1024)S(1)} %get-tuple-element.1089), channel_id=3, replica_groups=mesh['row'=8,'col'=4] {'row'}, dimensions={0}, use_global_device_ids=true | all-gather | bytes 147456 | tf_op jit(solution)/shard_map/all_gather | solution.py:13
  118.3 16.0 %while.180 = (s32[]{:T(128)}, f32[4,256]{1,0:T(4,128)S(1)}, f32[4,256]{1,0:T(4,128)S(1)}, f32[4096]{0:T(1024)S(1)}, f32[4096]{0:T(1024)S(1)}, /*index=5*/f32[4,2...) while((s32[]{:T(128)}, f32[4,256]{1,0:T(4,128)S(1)}, ...), condition=%wide.region_17.18_spmd, body=%wide.region_14.17_spmd.sunk | while | flops 547356160 | bytes 10676857 | solution.py:57
  118.4 3.2 fusion.83
  121.5 0.7 exponential_reduce_fusion.13
  122.4 3.2 fusion.83
  125.5 0.7 exponential_reduce_fusion.13
  126.4 3.2 fusion.83
  129.5 0.7 exponential_reduce_fusion.13
  130.4 3.2 fusion.83
  133.5 0.7 exponential_reduce_fusion.13
  134.4 13.2 %all-gather.8 = f32[4,1,1024]{2,1,0:T(1,128)S(1)} all-gather(f32[1,1,1024]{2,1,0:T(1,128)S(1)} %reshape.93), channel_id=1, replica_groups=mesh['row'=8,'col'=4] {'col'}, dimensions={0}, use_global_device_ids=true | all-gather | bytes 20480 | tf_op jit(solution)/shard_map/all_gather | solution.py:13
  147.6 13.2 %all-gather.9 = f32[4,1,1024]{2,1,0:T(1,128)S(1)} all-gather(f32[1,1,1024]{2,1,0:T(1,128)S(1)} %reshape.95), channel_id=1, replica_groups=mesh['row'=8,'col'=4] {'col'}, dimensions={0}, use_global_device_ids=true | all-gather | bytes 20480 | tf_op jit(solution)/shard_map/all_gather | solution.py:13
  161.0 15.2 %while.187 = (s32[]{:T(128)}, f32[4096]{0:T(1024)S(1)}, f32[4096]{0:T(1024)S(1)}, f32[4,256]{1,0:T(4,128)S(1)}, f32[4,256]{1,0:T(4,128)S(1)}, /*index=5*/f32[4,2...) while((s32[]{:T(128)}, f32[4096]{0:T(1024)S(1)}, ...), condition=%wide.region_23.24_spmd.clone, body=%wide.region_20.23_spmd.clone.sunk | while | flops 547381248 | bytes 10790527 | solution.py:77
  161.1 3.1 fusion.90
  164.9 3.1 fusion.90
  168.7 3.1 fusion.90
  172.5 3.1 fusion.90
  176.2 9.3 %all-gather.2 = f32[32768]{0:T(1024)S(1)} all-gather(f32[4096]{0:T(1024)S(1)} %get-tuple-element.1096), channel_id=4, replica_groups=mesh['row'=8,'col'=4] {'row'}, dimensions={0}, use_global_device_ids=true | all-gather | bytes 147456 | tf_op jit(solution)/shard_map/all_gather | solution.py:13
  185.6 8.3 %all-gather.3 = f32[32768]{0:T(1024)S(1)} all-gather(f32[4096]{0:T(1024)S(1)} %get-tuple-element.1097), channel_id=5, replica_groups=mesh['row'=8,'col'=4] {'row'}, dimensions={0}, use_global_device_ids=true | all-gather | bytes 147456 | tf_op jit(solution)/shard_map/all_gather | solution.py:13
  194.5 16.0 %while.183 = (s32[]{:T(128)}, f32[4,256]{1,0:T(4,128)S(1)}, f32[4,256]{1,0:T(4,128)S(1)}, f32[4096]{0:T(1024)S(1)}, f32[4096]{0:T(1024)S(1)}, /*index=5*/f32[4,2...) while((s32[]{:T(128)}, f32[4,256]{1,0:T(4,128)S(1)}, ...), condition=%wide.region_29.30_spmd, body=%wide.region_26.29_spmd.sunk | while | flops 547356160 | bytes 10676857 | solution.py:57
  194.6 3.2 fusion.85
  197.7 0.7 exponential_reduce_fusion.14
  198.6 3.2 fusion.85
  201.7 0.7 exponential_reduce_fusion.14
  202.6 3.2 fusion.85
  205.7 0.7 exponential_reduce_fusion.14
  206.6 3.2 fusion.85
  209.7 0.7 exponential_reduce_fusion.14
  210.6 13.2 %all-gather.10 = f32[4,1,1024]{2,1,0:T(1,128)S(1)} all-gather(f32[1,1,1024]{2,1,0:T(1,128)S(1)} %reshape.97), channel_id=1, replica_groups=mesh['row'=8,'col'=4] {'col'}, dimensions={0}, use_global_device_ids=true | all-gather | bytes 20480 | tf_op jit(solution)/shard_map/all_gather | solution.py:13
  223.8 13.2 %all-gather.11 = f32[4,1,1024]{2,1,0:T(1,128)S(1)} all-gather(f32[1,1,1024]{2,1,0:T(1,128)S(1)} %reshape.99), channel_id=1, replica_groups=mesh['row'=8,'col'=4] {'col'}, dimensions={0}, use_global_device_ids=true | all-gather | bytes 20480 | tf_op jit(solution)/shard_map/all_gather | solution.py:13
  237.2 0.6 fusion.52
  238.4 15.2 %while.188 = (s32[]{:T(128)}, f32[4096]{0:T(1024)S(1)}, f32[4096]{0:T(1024)S(1)}, f32[4,256]{1,0:T(4,128)S(1)}, f32[4,256]{1,0:T(4,128)S(1)}, /*index=5*/f32[4,2...) while((s32[]{:T(128)}, f32[4096]{0:T(1024)S(1)}, ...), condition=%wide.region_35.36_spmd.clone, body=%wide.region_32.35_spmd.clone.sunk | while | flops 547381248 | bytes 10790527 | solution.py:77
  238.4 3.1 fusion.93
  242.2 3.1 fusion.93
  246.0 3.1 fusion.93
  249.8 3.1 fusion.93
  253.6 9.2 %all-gather.4 = f32[32768]{0:T(1024)S(1)} all-gather(f32[4096]{0:T(1024)S(1)} %get-tuple-element.1104), channel_id=6, replica_groups=mesh['row'=8,'col'=4] {'row'}, dimensions={0}, use_global_device_ids=true | all-gather | bytes 147456 | tf_op jit(solution)/shard_map/all_gather | solution.py:13
  262.8 8.3 %all-gather.5 = f32[32768]{0:T(1024)S(1)} all-gather(f32[4096]{0:T(1024)S(1)} %get-tuple-element.1105), channel_id=7, replica_groups=mesh['row'=8,'col'=4] {'row'}, dimensions={0}, use_global_device_ids=true | all-gather | bytes 147456 | tf_op jit(solution)/shard_map/all_gather | solution.py:13
  271.7 1.3 fusion.51
  274.3 39.1 %psum.7 = f32[]{:T(128)} all-reduce(f32[]{:T(128)S(6)} %add.464), channel_id=1, replica_groups=mesh['row'=8,'col'=4] {'row','col'}, use_global_device_ids=true, to_apply=%region_40.41 | all-reduce | flops 1 | bytes 8 | tf_op jit(solution)/shard_map/psum | solution.py:85
  (203 shorter events, 12.0 us)
Async XLA Ops:
  7.2 33.2 %all-gather.14.cloned.1.call-start = ((), (), s32[]{:S(2)}) async-start(), calls=%async_computation | async-start | bytes 2359296 | tf_op jit(solution)/shard_map/all_gather | solution.py:35
  85.0 33.3 %copy-start.1 = (f32[4096]{0:T(1024)S(1)}, f32[4096]{0:T(1024)}, u32[]{:S(2)}) copy-start(f32[4096]{0:T(1024)} %get-tuple-element.2387) | copy-start | bytes 49156
  237.8 0.6 copy-start
Sparse Core Ops, SparseCore 0:
  9.9 30.4 all-gather.13
where the time goes:
time: 322 us; the launch traced here: 320 us
  blocking collectives  171 us (53%)
  matrix products  75.1 us (23%)
  waiting for transfers between devices  31.2 us (10%)
  other arithmetic  22 us (7%)
  between operations  15.7 us (5%)
  local copies, waits for them, and re-layouts  3.61 us (1%)
    all_gather x12, blocking collectives, combined_all(): everything = jax.tree.map(lambda part: lax.all_gather(part, axis), value)  132 us
    dot_general x24, matrix products, cost_block(): lax.dot_general(points_a, points_b, (((1,), (1,)), ((), ())), preferred_e...  75.1 us
    psum x1, blocking collectives, body(): mean_potentials = lax.psum(local, ('row', 'col'))  39.1 us
    all_gather x1, waiting for transfers between devices, body(): targets = lax.all_gather(tgt_points, 'row', axis=0, tiled=True)  30.5 us
    reduce_sum x12, other arithmetic, row_pair(): return (top, jnp.sum(jnp.exp(terms - top[:, None]), axis=1))  8.61 us
    reduce_sum x12, other arithmetic, pair_step(): block_sum = jnp.sum(jnp.exp(terms - block_top[None, :]), axis=0)  7.15 us
  transfers between devices with their start and end apart: 1, of which 1 were waited for; matrix products, arithmetic and copies ran while one was open for 1% of the time, Pallas kernels for 0%

commit v1 on v0

v1 whole, which is shorter than its diff:
```python
import functools
import math

import jax
import jax.numpy as jnp
from jax import lax
from jax.experimental import pallas as pl
from jax.experimental.pallas import tpu as pltpu
from jax.sharding import PartitionSpec as P

ITERS = 3
entropy_weight = 0.1
LOG2E = math.log2(math.e)
SCALE = LOG2E / entropy_weight
LANES = 128
HIGHEST = lax.Precision.HIGHEST
MESH = pl.DeviceIdType.MESH


def to_col(row):
    return jnp.broadcast_to(row, (LANES, LANES)).T


def widen(col, width):
    return jnp.concatenate([col] * (width // LANES), axis=1)


def fold(x, op):
    parts = [x[:, k : k + LANES] for k in range(0, x.shape[1], LANES)]
    while len(parts) > 1:
        parts = [op(a, b) for a, b in zip(parts[::2], parts[1::2])] + parts[len(parts) & ~1 :]
    return parts[0]


def flip(index, bit):
    return index + bit - 2 * bit * (index // bit % 2)


def kernel(
    nrow, ncol, chunks,
    x_hbm, t_hbm, ls_ref, lm_ref,
    f_ref, g_ref, mean_ref,
    x_ref, gath, z_ref, pcol, mlane, glane, wlane, fbuf, gbuf, tbuf, hbuf,
    in_sem, blk_send, blk_recv, f_send, f_recv, g_send, g_recv, t_sem, h_sem,
):
    r, c = lax.axis_index("row"), lax.axis_index("col")
    sources, width = x_ref.shape
    targets = z_ref.shape[0]
    block = targets // nrow
    half = block // 2
    chunk = targets // chunks
    sub = min(256, block)

    load_t = pltpu.make_async_copy(t_hbm, gath.at[r], in_sem.at[0])
    load_x = pltpu.make_async_copy(x_hbm, x_ref, in_sem.at[1])
    load_t.start()
    load_x.start()

    barrier = pltpu.get_barrier_semaphore()
    for d in range(1, nrow):
        pl.semaphore_signal(barrier, inc=1, device_id=(lax.rem(r + d, nrow), c), device_id_type=MESH)
    for d in range(1, ncol):
        pl.semaphore_signal(barrier, inc=1, device_id=(r, lax.rem(c + d, ncol)), device_id_type=MESH)
    load_t.wait()
    pl.semaphore_wait(barrier, nrow + ncol - 2)

    sent = []

    def send_block(slot, part, to):
        rows = pl.ds(part * half, half)
        copy = pltpu.make_async_remote_copy(
            src_ref=gath.at[slot, rows],
            dst_ref=gath.at[slot, rows],
            send_sem=blk_send.at[len(sent)],
            recv_sem=blk_recv.at[slot, part],
            device_id=(to, c),
            device_id_type=MESH,
        )
        copy.start()
        sent.append(copy)

    def wait_block(slot, part):
        rows = pl.ds(part * half, half)
        pltpu.make_async_copy(gath.at[slot, rows], gath.at[slot, rows], blk_recv.at[slot, part]).wait()

    if nrow == 8:
        p1, px, py = flip(r, 1), flip(r, 2), flip(r, 4)
        send_block(r, 0, px)
        send_block(r, 1, py)
        send_block(r, 1, px)
        send_block(r, 0, py)
        send_block(r, 0, p1)
        send_block(r, 1, p1)
    else:
        for d in range(1, nrow):
            for part in range(2):
                send_block(r, part, lax.rem(r + d, nrow))

    load_x.wait()
    x32 = x_ref[...].astype(jnp.float32)
    qx = lax.dot_general(
        jnp.ones((8, width), jnp.float32), x32 * x32, (((1,), (1,)), ((), ())),
        precision=HIGHEST, preferred_element_type=jnp.float32,
    )[0:1] * (SCALE / width)
    ls2 = ls_ref[...] * LOG2E
    els = jnp.exp2(ls2)

    def row_block(slot, carry):
        def piece(k, carry):
            top, total = carry
            start = pl.multiple_of(slot * block + k * sub, sub)
            pts = gath[slot, pl.ds(pl.multiple_of(k * sub, sub), sub), :]
            product = lax.dot_general(
                pts, x_ref[...], (((1,), (1,)), ((), ())), preferred_element_type=jnp.float32
            )
            p32 = pts.astype(jnp.float32)
            sq = jnp.sum(p32 * p32, axis=1, keepdims=True) * (SCALE / width)
            cols = [
                to_col(lm_ref[:, pl.ds(pl.multiple_of(start + b, LANES), LANES)])
                for b in range(0, sub, LANES)
            ]
            shift = jnp.concatenate(cols, axis=0) * LOG2E - jnp.broadcast_to(sq, (sub, LANES))
            z = product * (2.0 * SCALE / width) + widen(shift, sources)
            z_ref[pl.ds(start, sub), :] = z
            new_top = jnp.maximum(top, jnp.max(z.reshape(sub // 8, 8, sources), axis=0))
            again = z_ref[pl.ds(start, sub), :].reshape(sub // 8, 8, sources)
            part = jnp.sum(jnp.exp2(again - new_top[None]), axis=0)
            return new_top, total * jnp.exp2(top - new_top) + part

        return lax.fori_loop(0, block // sub, piece, carry)

    carry = (jnp.full((8, sources), -3.0e38, jnp.float32), jnp.zeros((8, sources), jnp.float32))
    carry = row_block(r, carry)
    if nrow == 8:
        wait_block(p1, 0)
        wait_block(p1, 1)
        carry = row_block(p1, carry)
        wait_block(px, 0)
        send_block(px, 0, py)
        send_block(px, 0, p1)
        wait_block(py, 1)
        send_block(py, 1, px)
        send_block(py, 1, p1)
        wait_block(px, 1)
        send_block(px, 1, p1)
        wait_block(py, 0)
        send_block(py, 0, p1)
        pd = flip(px, 4)
        order = [px, py, flip(px, 1), flip(py, 1)]
        carry = row_block(px, carry)
        carry = row_block(py, carry)
        for slot in order[2:]:
            wait_block(slot, 0)
            wait_block(slot, 1)
            carry = row_block(slot, carry)
        for part in range(2):
            wait_block(pd, part)
            send_block(pd, part, p1)
        carry = row_block(pd, carry)
        last = flip(pd, 1)
        wait_block(last, 0)
        wait_block(last, 1)
        carry = row_block(last, carry)
    else:
        for d in range(1, nrow):
            slot = lax.rem(r + nrow - d, nrow)
            wait_block(slot, 0)
            wait_block(slot, 1)
            carry = row_block(slot, carry)

    def send_f(k, buf, send_sem, recv_sem):
        for d in range(1, ncol):
            pltpu.make_async_remote_copy(
                src_ref=buf.at[k, c], dst_ref=buf.at[k, c], send_sem=send_sem.at[k],
                recv_sem=recv_sem.at[k], device_id=(r, lax.rem(c + d, ncol)), device_id_type=MESH,
            ).start()

    def send_row(k, buf, send_sem, recv_sem):
        for d in range(1, nrow):
            pltpu.make_async_remote_copy(
                src_ref=buf.at[k, r], dst_ref=buf.at[k, r], send_sem=send_sem.at[k],
                recv_sem=recv_sem.at[k], device_id=(lax.rem(r + d, nrow), c), device_id_type=MESH,
            ).start()

    def wait_all(k, buf, sem):
        part = buf.at[k, pl.ds(0, buf.shape[1] - 1)]
        pltpu.make_async_copy(part, part, sem.at[k]).wait()

    def total_of(k, buf):
        return functools.reduce(lambda a, b: a + b, [buf[k, d] for d in range(buf.shape[1])])

    def lse_of(k, buf):
        parts = [buf[k, d] for d in range(buf.shape[1])]
        top = functools.reduce(jnp.maximum, parts)
        return top + jnp.log2(functools.reduce(lambda a, b: a + b, [jnp.exp2(p - top) for p in parts]))

    top8, total8 = carry
    top = jnp.max(top8, axis=0, keepdims=True)
    total = jnp.sum(total8 * jnp.exp2(top8 - top), axis=0, keepdims=True)
    fbuf[0, c] = top + jnp.log2(total)
    send_f(0, fbuf, f_send, f_recv)
    wait_all(0, fbuf, f_recv)
    first_f = -lse_of(0, fbuf)
    shift = ls2 + first_f

    def compact(start):
        rows = [
            jnp.sum(pcol[pl.ds(pl.multiple_of(start + b, LANES), LANES), :].T, axis=0, keepdims=True)
            for b in range(0, chunk, LANES)
        ]
        return jnp.concatenate(rows, axis=1)

    def col_first(k):
        start = pl.multiple_of(k * chunk, chunk)

        def piece(i, unused):
            rows = pl.ds(pl.multiple_of(start + i * LANES, LANES), LANES)
            high = jnp.max(fold(z_ref[rows, :] + shift, jnp.maximum), axis=1, keepdims=True)
            high = jnp.broadcast_to(high, (LANES, LANES))
            e = jnp.exp2(z_ref[rows, :] + shift - widen(high, sources))
            z_ref[rows, :] = e
            pcol[rows, :] = fold(e, jnp.add)
            lane = pl.ds(pl.multiple_of(start + i * LANES, LANES), LANES)
            mlane[:, lane] = high.T[0:1, :]
            return unused

        lax.fori_loop(0, chunk // LANES, piece, 0)
        lane = pl.ds(start, chunk)
        gbuf[k, r] = mlane[:, lane] + jnp.log2(compact(start))
        send_row(k, gbuf, g_send, g_recv)

    for k in range(chunks):
        col_first(k)

    def row_again(k, it, acc):
        slot = (it - 1) * chunks + k
        start = k * chunk
        lane = pl.ds(start, chunk)
        wait_all(slot, gbuf, g_recv)
        if it == 1:
            lse = lse_of(slot, gbuf)
            glane[:, lane] = lse
            wlane[0, :, lane] = jnp.exp2(mlane[:, lane] - lse)
            w = wlane[0, :, lane] * jnp.exp2(lm_ref[:, lane] * LOG2E)
            wlane[1, :, lane] = w
        else:
            w = wlane[1, :, lane] / total_of(slot, gbuf)
        wlane[2, :, lane] = w

        def piece(i, acc):
            lane = pl.ds(pl.multiple_of(start + i * LANES, LANES), LANES)
            wc = to_col(wlane[2, :, lane])
            product = z_ref[lane, :] * widen(wc, sources)
            return acc + jnp.sum(product.reshape(LANES // 8, 8, sources), axis=0)

        return lax.fori_loop(0, chunk // LANES, piece, acc)

    def col_again(k, it, u):
        start = k * chunk
        slot = it * chunks + k

        def piece(i, unused):
            rows = pl.ds(pl.multiple_of(start + i * LANES, LANES), LANES)
            pcol[rows, :] = fold(z_ref[rows, :] * u, jnp.add)
            return unused

        lax.fori_loop(0, chunk // LANES, piece, 0)
        gbuf[slot, r] = wlane[0, :, pl.ds(start, chunk)] * compact(start)
        send_row(slot, gbuf, g_send, g_recv)

    sources_all = sources * nrow
    targets_all = targets * ncol
    for it in range(1, ITERS):
        acc = jnp.zeros((8, sources), jnp.float32)
        for k in range(chunks):
            acc = row_again(k, it, acc)
        fbuf[it, c] = jnp.sum(acc, axis=0, keepdims=True)
        send_f(it, fbuf, f_send, f_recv)
        wait_all(it, fbuf, f_recv)
        rowsum = total_of(it, fbuf)
        u = els / rowsum
        if it == ITERS - 1:
            f = (first_f + qx + ls2 - jnp.log2(rowsum)) * (1.0 / SCALE)
            f_ref[...] = f
            tbuf[0, r] = jnp.broadcast_to(
                jnp.sum(f, axis=1, keepdims=True) * (1.0 / (sources_all * ncol)), (1, LANES)
            )
            send_row(0, tbuf, t_sem.at[0], t_sem.at[1])
        for k in range(chunks):
            col_again(k, it, u)

    acc = jnp.zeros((1, LANES), jnp.float32)
    for k in range(chunks):
        slot = (ITERS - 1) * chunks + k
        lane = pl.ds(k * chunk, chunk)
        wait_all(slot, gbuf, g_recv)
        g = (lm_ref[:, lane] * LOG2E - glane[:, lane] - jnp.log2(total_of(slot, gbuf))) * (1.0 / SCALE)
        g_ref[:, lane] = g
        acc = acc + fold(g, jnp.add)
    wait_all(0, tbuf, t_sem.at[1])
    hbuf[0, c] = total_of(0, tbuf) + jnp.broadcast_to(
        jnp.sum(acc, axis=1, keepdims=True) * (1.0 / targets_all), (1, LANES)
    )
    send_f(0, hbuf, h_sem.at[0], h_sem.at[1])
    wait_all(0, hbuf, h_sem.at[1])
    mean_ref[...] = total_of(0, hbuf)

    for copy in sent:
        copy.wait_send()
    for it in range(ITERS):
        wait_all(it, fbuf, f_send)
    for slot in range(ITERS * chunks):
        wait_all(slot, gbuf, g_send)
    wait_all(0, tbuf, t_sem.at[0])
    wait_all(0, hbuf, h_sem.at[0])


def body(nrow, ncol, src_points, tgt_points, log_src_mass, log_tgt_mass):
    sources, width = src_points.shape
    block = tgt_points.shape[0]
    targets = block * nrow
    chunks = 4
    chunk = targets // chunks
    f32 = jnp.float32
    vmem = pl.BlockSpec(memory_space=pltpu.VMEM)
    hbm = pl.BlockSpec(memory_space=pl.ANY)
    dma = pltpu.SemaphoreType.DMA
    sends = 14 if nrow == 8 else 2 * (nrow - 1)
    f, g, mean = pl.pallas_call(
        functools.partial(kernel, nrow, ncol, chunks),
        out_shape=(
            jax.ShapeDtypeStruct((1, sources), f32),
            jax.ShapeDtypeStruct((1, targets), f32),
            jax.ShapeDtypeStruct((1, LANES), f32),
        ),
        in_specs=[hbm, hbm, vmem, vmem],
        out_specs=(vmem, vmem, vmem),
        scratch_shapes=[
            pltpu.VMEM((sources, width), jnp.bfloat16),
            pltpu.VMEM((nrow, block, width), jnp.bfloat16),
            pltpu.VMEM((targets, sources), f32),
            pltpu.VMEM((targets, LANES), f32),
            pltpu.VMEM((1, targets), f32),
            pltpu.VMEM((1, targets), f32),
            pltpu.VMEM((3, 1, targets), f32),
            pltpu.VMEM((ITERS, ncol, 1, sources), f32),
            pltpu.VMEM((ITERS * chunks, nrow, 1, chunk), f32),
            pltpu.VMEM((1, nrow, 1, LANES), f32),
            pltpu.VMEM((1, ncol, 1, LANES), f32),
            dma((2,)),
            dma((sends,)),
            dma((nrow, 2)),
            dma((ITERS,)),
            dma((ITERS,)),
            dma((ITERS * chunks,)),
            dma((ITERS * chunks,)),
            dma((2, 1)),
            dma((2, 1)),
        ],
        compiler_params=pltpu.CompilerParams(
            collective_id=0, has_side_effects=True, vmem_limit_bytes=60 * 1024 * 1024
        ),
        name="sinkhorn",
    )(src_points, tgt_points, log_src_mass.reshape(1, -1), log_tgt_mass.reshape(1, -1))
    return f.reshape(-1), g.reshape(-1), mean[0, 0]


def solution(mesh):
    return jax.shard_map(
        functools.partial(body, mesh.shape["row"], mesh.shape["col"]),
        mesh=mesh,
        in_specs=(P("row", None), P(("col", "row"), None), P("row"), P("col")),
        out_specs=(P("row"), P("col"), P()),
        check_vma=False,
    )
```

time: 322 us -> 62.5 us (0.19)
  blocking collectives: 171 us -> 0 us
  matrix products: 75.1 us -> 0 us
  Pallas kernels: 0 us -> 58.4 us
  waiting for transfers between devices: 31.2 us -> 0 us
  other arithmetic: 22 us -> 0 us
  between operations: 15.7 us -> 1.81 us
    all_gather x12 -> x0, blocking collectives: 132 us -> none  [combined_all(): everything = jax.tree.map(lambda part: lax.all_gather(part, axis), value)]
    dot_general x24 -> x0, matrix products: 75.1 us -> none  [cost_block(): lax.dot_general(points_a, points_b, (((1,), (1,)), ((), ())), preferred_e...]
    pallas_call x0 -> x1, Pallas kernels: none -> 58.4 us  [body(): pl.pallas_call(functools.partial(kernel, nrow, ncol, chunks), out_shape=(...]
    psum x1 -> x0, blocking collectives: 39.1 us -> none  [body(): mean_potentials = lax.psum(local, ('row', 'col'))]
    all_gather x1 -> x0, waiting for transfers between devices: 30.5 us -> none  [body(): targets = lax.all_gather(tgt_points, 'row', axis=0, tiled=True)]
    reduce_sum x28 -> x0, other arithmetic: 21.1 us -> none  [the longest x12 8.61 us: row_pair(): return (top, jnp.sum(jnp.exp(terms - top[:, None]), axis=1))]
  transfers between devices with their start and end apart: 1 -> 0, of which waited for: 1 -> 0; matrix products, arithmetic and copies ran while one was open for 1% -> 0% of each run, Pallas kernels for 0% -> 0%
where the time goes in v1:
time: 62.5 us; the launch traced here: 62.1 us
  Pallas kernels  58.4 us (93%)
  local copies, waits for them, and re-layouts  1.89 us (3%)
  between operations  1.81 us (3%)
    pallas_call x1, Pallas kernels, body(): pl.pallas_call(functools.partial(kernel, nrow, ncol, chunks), out_shape=(...  58.4 us
    unnamed x6, local copies, waits for them, and re-layouts  1.89 us

profile of v1, /device:TPU:0, one launch (start us, length us, event | category | flops | bytes accessed | tf_op | source)
XLA Modules:
  0.0 62.1 jit_solution(1044225439918809398)
XLA Ops:
  0.6 58.4 %sinkhorn.1 = (f32[1,1024]{1,0:T(1,128)}, f32[1,4096]{1,0:T(1,128)}, f32[1,128]{1,0:T(1,128)}) custom-call(bf16[1024,256]{1,0:T(8,128)(2,1)} %x_hbm.1, bf16[512,256]{1,0:T(8,128)(2,1)} %t_hbm.1, f32[1,1024]{1,0:T(1,128)} %bitcast.8, f32[1,4096]{1,0:T(1,128)} %bitcast.6), custom_call_target="tpu_custom_call" | custom-call | tf_op jit(solution)/shard_map/sinkhorn/pallas_call | solution.py:329
  59.1 0.0 copy-start
  59.1 1.3 %copy.10 = f32[1024]{0:T(1024)} copy(f32[1024]{0:T(1024)} %bitcast.9) | data formatting | bytes 8192
  60.4 0.0 copy-done
  60.4 0.0 copy-start.1
  60.4 0.6 copy.11
  61.0 0.0 copy-done.1
Async XLA Ops:
  59.1 1.3 %copy-start = (f32[1,4096]{1,0:T(1,128)S(1)}, f32[1,4096]{1,0:T(1,128)}, u32[]{:S(2)}) copy-start(f32[1,4096]{1,0:T(1,128)} %get-tuple-element.7) | copy-start | bytes 49156
  60.4 0.6 copy-start.1

commit v2 on v1

--- a/solution.py
+++ b/solution.py
@@ -40,7 +40,7 @@
     nrow, ncol, chunks,
     x_hbm, t_hbm, ls_ref, lm_ref,
     f_ref, g_ref, mean_ref,
-    x_ref, gath, z_ref, pcol, mlane, glane, wlane, fbuf, gbuf, tbuf, hbuf,
+    x_ref, gath, z_ref, mlane, glane, wlane, fbuf, gbuf, tbuf, hbuf,
     in_sem, blk_send, blk_recv, f_send, f_recv, g_send, g_recv, t_sem, h_sem,
 ):
     r, c = lax.axis_index("row"), lax.axis_index("col")
@@ -49,7 +49,8 @@
     block = targets // nrow
     half = block // 2
     chunk = targets // chunks
-    sub = min(256, block)
+    wide, wide_first = min(512, chunk), min(256, chunk)
+    sub = min(256, half)
 
     load_t = pltpu.make_async_copy(t_hbm, gath.at[r], in_sem.at[0])
     load_x = pltpu.make_async_copy(x_hbm, x_ref, in_sem.at[1])
@@ -57,10 +58,10 @@
     load_x.start()
 
     barrier = pltpu.get_barrier_semaphore()
+    for d in range(1, ncol):
+        pl.semaphore_signal(barrier, inc=1, device_id=(r, lax.rem(c + d, ncol)), device_id_type=MESH)
     for d in range(1, nrow):
         pl.semaphore_signal(barrier, inc=1, device_id=(lax.rem(r + d, nrow), c), device_id_type=MESH)
-    for d in range(1, ncol):
-        pl.semaphore_signal(barrier, inc=1, device_id=(r, lax.rem(c + d, ncol)), device_id_type=MESH)
     load_t.wait()
     pl.semaphore_wait(barrier, nrow + ncol - 2)
 
@@ -105,11 +106,13 @@
     ls2 = ls_ref[...] * LOG2E
     els = jnp.exp2(ls2)
 
-    def row_block(slot, carry):
+    def row_half(slot, part, carry):
+        base = part * half
+
         def piece(k, carry):
             top, total = carry
-            start = pl.multiple_of(slot * block + k * sub, sub)
-            pts = gath[slot, pl.ds(pl.multiple_of(k * sub, sub), sub), :]
+            start = pl.multiple_of(slot * block + base + k * sub, sub)
+            pts = gath[slot, pl.ds(pl.multiple_of(base + k * sub, sub), sub), :]
             product = lax.dot_general(
                 pts, x_ref[...], (((1,), (1,)), ((), ())), preferred_element_type=jnp.float32
             )
@@ -127,46 +130,47 @@
             part = jnp.sum(jnp.exp2(again - new_top[None]), axis=0)
             return new_top, total * jnp.exp2(top - new_top) + part
 
-        return lax.fori_loop(0, block // sub, piece, carry)
+        return lax.fori_loop(0, half // sub, piece, carry)
 
     carry = (jnp.full((8, sources), -3.0e38, jnp.float32), jnp.zeros((8, sources), jnp.float32))
-    carry = row_block(r, carry)
+    def arrived(slot, part, carry, *onward):
+        wait_block(slot, part)
+        for to in onward:
+            send_block(slot, part, to)
+        return row_half(slot, part, carry)
+
+    carry = row_half(r, 1, row_half(r, 0, carry))
     if nrow == 8:
-        wait_block(p1, 0)
-        wait_block(p1, 1)
-        carry = row_block(p1, carry)
+        carry = arrived(p1, 0, carry)
+        carry = arrived(p1, 1, carry)
         wait_block(px, 0)
         send_block(px, 0, py)
         send_block(px, 0, p1)
         wait_block(py, 1)
         send_block(py, 1, px)
         send_block(py, 1, p1)
-        wait_block(px, 1)
-        send_block(px, 1, p1)
-        wait_block(py, 0)
-        send_block(py, 0, p1)
-        pd = flip(px, 4)
-        order = [px, py, flip(px, 1), flip(py, 1)]
-        carry = row_block(px, carry)
-        carry = row_block(py, carry)
-        for slot in order[2:]:
-            wait_block(slot, 0)
-            wait_block(slot, 1)
-            carry = row_block(slot, carry)
+        carry = row_half(px, 0, carry)
+        carry = row_half(py, 1, carry)
+        px1, py1, pd = flip(px, 1), flip(py, 1), flip(px, 4)
+        carry = arrived(px1, 0, carry)
+        carry = arrived(px, 1, carry, p1)
+        carry = arrived(py, 0, carry, p1)
+        carry = arrived(py1, 1, carry)
+        carry = arrived(px1, 1, carry)
         for part in range(2):
             wait_block(pd, part)
             send_block(pd, part, p1)
-        carry = row_block(pd, carry)
+        carry = arrived(py1, 0, carry)
+        carry = row_half(pd, 0, carry)
+        carry = row_half(pd, 1, carry)
         last = flip(pd, 1)
-        wait_block(last, 0)
-        wait_block(last, 1)
-        carry = row_block(last, carry)
+        carry = arrived(last, 0, carry)
+        carry = arrived(last, 1, carry)
     else:
         for d in range(1, nrow):
             slot = lax.rem(r + nrow - d, nrow)
-            wait_block(slot, 0)
-            wait_block(slot, 1)
-            carry = row_block(slot, carry)
+            for part in range(2):
+                carry = arrived(slot, part, carry)
 
     def send_f(k, buf, send_sem, recv_sem):
         for d in range(1, ncol):
@@ -203,30 +207,27 @@
     first_f = -lse_of(0, fbuf)
     shift = ls2 + first_f
 
-    def compact(start):
-        rows = [
-            jnp.sum(pcol[pl.ds(pl.multiple_of(start + b, LANES), LANES), :].T, axis=0, keepdims=True)
-            for b in range(0, chunk, LANES)
-        ]
-        return jnp.concatenate(rows, axis=1)
+    def sum_rows(p):
+        return jnp.sum(p.T, axis=0, keepdims=True)
 
     def col_first(k):
-        start = pl.multiple_of(k * chunk, chunk)
+        start = k * chunk
 
         def piece(i, unused):
-            rows = pl.ds(pl.multiple_of(start + i * LANES, LANES), LANES)
-            high = jnp.max(fold(z_ref[rows, :] + shift, jnp.maximum), axis=1, keepdims=True)
-            high = jnp.broadcast_to(high, (LANES, LANES))
-            e = jnp.exp2(z_ref[rows, :] + shift - widen(high, sources))
-            z_ref[rows, :] = e
-            pcol[rows, :] = fold(e, jnp.add)
-            lane = pl.ds(pl.multiple_of(start + i * LANES, LANES), LANES)
-            mlane[:, lane] = high.T[0:1, :]
+            base = pl.multiple_of(i * wide_first, wide_first)
+            for b in range(0, wide_first, LANES):
+                rows = pl.ds(pl.multiple_of(start + base + b, LANES), LANES)
+                high = jnp.max(fold(z_ref[rows, :] + shift, jnp.maximum), axis=1, keepdims=True)
+                high = jnp.broadcast_to(high, (LANES, LANES))
+                e = jnp.exp2(z_ref[rows, :] + shift - widen(high, sources))
+                z_ref[rows, :] = e
+                row = high.T[0:1, :]
+                mlane[:, rows] = row
+                lane = pl.ds(pl.multiple_of(base + b, LANES), LANES)
+                gbuf[k, r, :, lane] = row + jnp.log2(sum_rows(fold(e, jnp.add)))
             return unused
 
-        lax.fori_loop(0, chunk // LANES, piece, 0)
-        lane = pl.ds(start, chunk)
-        gbuf[k, r] = mlane[:, lane] + jnp.log2(compact(start))
+        lax.fori_loop(0, chunk // wide_first, piece, 0)
         send_row(k, gbuf, g_send, g_recv)
 
     for k in range(chunks):
@@ -248,24 +249,29 @@
         wlane[2, :, lane] = w
 
         def piece(i, acc):
-            lane = pl.ds(pl.multiple_of(start + i * LANES, LANES), LANES)
-            wc = to_col(wlane[2, :, lane])
-            product = z_ref[lane, :] * widen(wc, sources)
-            return acc + jnp.sum(product.reshape(LANES // 8, 8, sources), axis=0)
-
-        return lax.fori_loop(0, chunk // LANES, piece, acc)
+            for b in range(0, wide, LANES):
+                lane = pl.ds(pl.multiple_of(start + i * wide + b, LANES), LANES)
+                wc = to_col(wlane[2, :, lane])
+                product = z_ref[lane, :] * widen(wc, sources)
+                acc = acc + jnp.sum(product.reshape(LANES // 8, 8, sources), axis=0)
+            return acc
+
+        return lax.fori_loop(0, chunk // wide, piece, acc)
 
     def col_again(k, it, u):
         start = k * chunk
         slot = it * chunks + k
 
         def piece(i, unused):
-            rows = pl.ds(pl.multiple_of(start + i * LANES, LANES), LANES)
-            pcol[rows, :] = fold(z_ref[rows, :] * u, jnp.add)
+            base = pl.multiple_of(i * wide, wide)
+            for b in range(0, wide, LANES):
+                rows = pl.ds(pl.multiple_of(start + base + b, LANES), LANES)
+                lane = pl.ds(pl.multiple_of(base + b, LANES), LANES)
+                sums = sum_rows(fold(z_ref[rows, :] * u, jnp.add))
+                gbuf[slot, r, :, lane] = wlane[0, :, rows] * sums
             return unused
 
-        lax.fori_loop(0, chunk // LANES, piece, 0)
-        gbuf[slot, r] = wlane[0, :, pl.ds(start, chunk)] * compact(start)
+        lax.fori_loop(0, chunk // wide, piece, 0)
         send_row(slot, gbuf, g_send, g_recv)
 
     sources_all = sources * nrow
@@ -339,7 +345,6 @@
             pltpu.VMEM((sources, width), jnp.bfloat16),
             pltpu.VMEM((nrow, block, width), jnp.bfloat16),
             pltpu.VMEM((targets, sources), f32),
-            pltpu.VMEM((targets, LANES), f32),
             pltpu.VMEM((1, targets), f32),
             pltpu.VMEM((1, targets), f32),
             pltpu.VMEM((3, 1, targets), f32),

time: 62.5 us -> 58.7 us (0.939)
  Pallas kernels: 58.4 us -> 54.7 us
    pallas_call x1, Pallas kernels: 58.4 us -> 54.7 us  [body(): pl.pallas_call(functools.partial(kernel, nrow, ncol, chunks), out_shape=(...]
where the time goes in v2:
time: 58.7 us; the launch traced here: 58.4 us
  Pallas kernels  54.7 us (93%)
  local copies, waits for them, and re-layouts  1.89 us (3%)
  between operations  1.82 us (3%)
    pallas_call x1, Pallas kernels, body(): pl.pallas_call(functools.partial(kernel, nrow, ncol, chunks), out_shape=(...  54.7 us
    unnamed x6, local copies, waits for them, and re-layouts  1.89 us

profile of v2, /device:TPU:0, one launch (start us, length us, event | category | flops | bytes accessed | tf_op | source)
XLA Modules:
  0.0 58.4 jit_solution(14913275372914208155)
XLA Ops:
  0.6 54.7 %sinkhorn.1 = (f32[1,1024]{1,0:T(1,128)}, f32[1,4096]{1,0:T(1,128)}, f32[1,128]{1,0:T(1,128)}) custom-call(bf16[1024,256]{1,0:T(8,128)(2,1)} %x_hbm.1, bf16[512,256]{1,0:T(8,128)(2,1)} %t_hbm.1, f32[1,1024]{1,0:T(1,128)} %bitcast.8, f32[1,4096]{1,0:T(1,128)} %bitcast.6), custom_call_target="tpu_custom_call" | custom-call | tf_op jit(solution)/shard_map/sinkhorn/pallas_call | solution.py:335
  55.3 0.0 copy-start
  55.3 1.3 %copy.10 = f32[1024]{0:T(1024)} copy(f32[1024]{0:T(1024)} %bitcast.9) | data formatting | bytes 8192
  56.6 0.0 copy-done
  56.6 0.0 copy-start.1
  56.6 0.6 %copy.11 = f32[4096]{0:T(1024)} copy(f32[4096]{0:T(1024)S(1)} %bitcast.7) | data formatting | bytes 32768
  57.2 0.0 copy-done.1
Async XLA Ops:
  55.3 1.3 %copy-start = (f32[1,4096]{1,0:T(1,128)S(1)}, f32[1,4096]{1,0:T(1,128)}, u32[]{:S(2)}) copy-start(f32[1,4096]{1,0:T(1,128)} %get-tuple-element.7) | copy-start | bytes 49156
  56.6 0.6 %copy-start.1 = (f32[1,128]{1,0:T(1,128)S(1)}, f32[1,128]{1,0:T(1,128)}, u32[]{:S(2)}) copy-start(f32[1,128]{1,0:T(1,128)} %get-tuple-element.8) | copy-start | bytes 1540

commit v3 on v2

--- a/solution.py
+++ b/solution.py
@@ -38,10 +38,10 @@
 
 def kernel(
     nrow, ncol, chunks,
-    x_hbm, t_hbm, ls_ref, lm_ref,
-    f_ref, g_ref, mean_ref,
-    x_ref, gath, z_ref, mlane, glane, wlane, fbuf, gbuf, tbuf, hbuf,
-    in_sem, blk_send, blk_recv, f_send, f_recv, g_send, g_recv, t_sem, h_sem,
+    x_hbm, t_hbm, ls_hbm, lm_hbm,
+    f_hbm, g_hbm, mean_hbm,
+    ls_ref, lm_ref, f_ref, g_ref, mean_ref, x_ref, gath, z_ref, mlane, glane, wlane, fbuf, gbuf, tbuf, hbuf,
+    in_sem, out_sem, blk_send, blk_recv, f_send, f_recv, g_send, g_recv, t_sem, h_sem,
 ):
     r, c = lax.axis_index("row"), lax.axis_index("col")
     sources, width = x_ref.shape
@@ -54,8 +54,15 @@
 
     load_t = pltpu.make_async_copy(t_hbm, gath.at[r], in_sem.at[0])
     load_x = pltpu.make_async_copy(x_hbm, x_ref, in_sem.at[1])
-    load_t.start()
-    load_x.start()
+    load_ls = pltpu.make_async_copy(ls_hbm, ls_ref, in_sem.at[2])
+    load_lm = pltpu.make_async_copy(lm_hbm, lm_ref, in_sem.at[3])
+    loads = [load_t, load_x, load_ls, load_lm]
+    for copy in loads:
+        copy.start()
+    stores = [
+        pltpu.make_async_copy(src, dst, out_sem.at[k])
+        for k, (src, dst) in enumerate([(f_ref, f_hbm), (g_ref, g_hbm), (mean_ref, mean_hbm)])
+    ]
 
     barrier = pltpu.get_barrier_semaphore()
     for d in range(1, ncol):
@@ -97,7 +104,8 @@
             for part in range(2):
                 send_block(r, part, lax.rem(r + d, nrow))
 
-    load_x.wait()
+    for copy in loads[1:]:
+        copy.wait()
     x32 = x_ref[...].astype(jnp.float32)
     qx = lax.dot_general(
         jnp.ones((8, width), jnp.float32), x32 * x32, (((1,), (1,)), ((), ())),
@@ -288,6 +296,7 @@
         if it == ITERS - 1:
             f = (first_f + qx + ls2 - jnp.log2(rowsum)) * (1.0 / SCALE)
             f_ref[...] = f
+            stores[0].start()
             tbuf[0, r] = jnp.broadcast_to(
                 jnp.sum(f, axis=1, keepdims=True) * (1.0 / (sources_all * ncol)), (1, LANES)
             )
@@ -308,8 +317,10 @@
         jnp.sum(acc, axis=1, keepdims=True) * (1.0 / targets_all), (1, LANES)
     )
     send_f(0, hbuf, h_sem.at[0], h_sem.at[1])
+    stores[1].start()
     wait_all(0, hbuf, h_sem.at[1])
     mean_ref[...] = total_of(0, hbuf)
+    stores[2].start()
 
     for copy in sent:
         copy.wait_send()
@@ -319,6 +330,8 @@
         wait_all(slot, gbuf, g_send)
     wait_all(0, tbuf, t_sem.at[0])
     wait_all(0, hbuf, h_sem.at[0])
+    for copy in stores:
+        copy.wait()
 
 
 def body(nrow, ncol, src_points, tgt_points, log_src_mass, log_tgt_mass):
@@ -328,7 +341,6 @@
     chunks = 4
     chunk = targets // chunks
     f32 = jnp.float32
-    vmem = pl.BlockSpec(memory_space=pltpu.VMEM)
     hbm = pl.BlockSpec(memory_space=pl.ANY)
     dma = pltpu.SemaphoreType.DMA
     sends = 14 if nrow == 8 else 2 * (nrow - 1)
@@ -339,9 +351,14 @@
             jax.ShapeDtypeStruct((1, targets), f32),
             jax.ShapeDtypeStruct((1, LANES), f32),
         ),
-        in_specs=[hbm, hbm, vmem, vmem],
-        out_specs=(vmem, vmem, vmem),
+        in_specs=[hbm] * 4,
+        out_specs=(hbm,) * 3,
         scratch_shapes=[
+            pltpu.VMEM((1, sources), f32),
+            pltpu.VMEM((1, targets), f32),
+            pltpu.VMEM((1, sources), f32),
+            pltpu.VMEM((1, targets), f32),
+            pltpu.VMEM((1, LANES), f32),
             pltpu.VMEM((sources, width), jnp.bfloat16),
             pltpu.VMEM((nrow, block, width), jnp.bfloat16),
             pltpu.VMEM((targets, sources), f32),
@@ -352,7 +369,8 @@
             pltpu.VMEM((ITERS * chunks, nrow, 1, chunk), f32),
             pltpu.VMEM((1, nrow, 1, LANES), f32),
             pltpu.VMEM((1, ncol, 1, LANES), f32),
-            dma((2,)),
+            dma((4,)),
+            dma((3,)),
             dma((sends,)),
             dma((nrow, 2)),
             dma((ITERS,)),

time: 58.7 us -> 57.9 us (0.986)
  Pallas kernels: 54.7 us -> 54 us
    pallas_call x1, Pallas kernels: 54.7 us -> 54 us  [body(): pl.pallas_call(functools.partial(kernel, nrow, ncol, chunks), out_shape=(...]
where the time goes in v3:
time: 57.9 us; the launch traced here: 57.7 us
  Pallas kernels  54 us (93%)
  local copies, waits for them, and re-layouts  1.89 us (3%)
  between operations  1.82 us (3%)
    pallas_call x1, Pallas kernels, body(): pl.pallas_call(functools.partial(kernel, nrow, ncol, chunks), out_shape=(...  54 us
    unnamed x6, local copies, waits for them, and re-layouts  1.89 us

profile of v3, /device:TPU:0, one launch (start us, length us, event | category | flops | bytes accessed | tf_op | source)
XLA Modules:
  0.0 57.7 jit_solution(15899056198032564452)
XLA Ops:
  0.6 54.0 %sinkhorn.1 = (f32[1,1024]{1,0:T(1,128)}, f32[1,4096]{1,0:T(1,128)}, f32[1,128]{1,0:T(1,128)}) custom-call(bf16[1024,256]{1,0:T(8,128)(2,1)} %x_hbm.1, bf16[512,256]{1,0:T(8,128)(2,1)} %t_hbm.1, f32[1,1024]{1,0:T(1,128)} %bitcast.8, f32[1,4096]{1,0:T(1,128)} %bitcast.6), custom_call_target="tpu_custom_call" | custom-call | tf_op jit(solution)/shard_map/sinkhorn/pallas_call | solution.py:347
  54.7 0.0 copy-start
  54.7 1.3 %copy.10 = f32[1024]{0:T(1024)} copy(f32[1024]{0:T(1024)} %bitcast.9) | data formatting | bytes 8192
  56.0 0.0 copy-done
  56.0 0.0 copy-start.1
  56.0 0.6 %copy.11 = f32[4096]{0:T(1024)} copy(f32[4096]{0:T(1024)S(1)} %bitcast.7) | data formatting | bytes 32768
  56.6 0.0 copy-done.1
Async XLA Ops:
  54.7 1.3 %copy-start = (f32[1,4096]{1,0:T(1,128)S(1)}, f32[1,4096]{1,0:T(1,128)}, u32[]{:S(2)}) copy-start(f32[1,4096]{1,0:T(1,128)} %get-tuple-element.7) | copy-start | bytes 49156
  56.0 0.6 %copy-start.1 = (f32[1,128]{1,0:T(1,128)S(1)}, f32[1,128]{1,0:T(1,128)}, u32[]{:S(2)}) copy-start(f32[1,128]{1,0:T(1,128)} %get-tuple-element.8) | copy-start | bytes 1540
